TPU v7x, 32 devices: a whole 2x2x4 slice. The times are simulated.
32 devices in a mesh: sta: 8 (over z, y), yr: 4 (over x, core).
Axes of the slice: x: 2, y: 2, z: 4, core: 2. Of those that a mesh axis runs over, the one named last changes fastest.
Arguments:
- temps: float32 [196608, 128], P(('sta', 'yr')), may hold values from -6 to 6
- day_bits: int32 [4, 196608], P(None, ('sta', 'yr')), may hold values from -2147483648 to 2147483646, as said below
- block_offset: int32 [196608], P(('sta', 'yr')), may hold values from 0 to 47
- block_counts: int32 [4, 2048], P('yr', 'sta'), may hold values from 0 to 48, as said below
- station_cell: int32 [2048], P('sta'), may hold values from 0 to 10367, as said below
Outputs:
- anomalies: float32 [196608, 128], P(('sta', 'yr'))
- climatology: float32 [10368, 384], P('sta')
Inputs may be any that keep to these rules, and one draw needn't show every extreme that they name: `day_bits`: bit i of word w of a block's column says whether day 32 * w + i of the block was observed. `block_counts`: for each year range and station shard, the counts of the shard's 256 stations sum to 6144; in each of them some station has 48. `station_cell`: the owner of cell c is c // 1296. Of the 256 stations of one shard at most 128 lie in cells of one owner, and one owner has exactly 128 stations of every shard.
All inputs are finite; a program needn't handle non-finite values.
Results may differ from a plain program's by a relative error of at most 0.0003.
Values sent between devices are 32-bit elements; how exact they have to be, the bound alone decides.
A program may use at most 128 MiB of HBM per device.

v0:
```python
import jax
import jax.numpy as jnp
from jax import lax
from jax.sharding import PartitionSpec as P

CELLS = 10368


CALENDAR = 365


def observed_days(packed, offsets):
    day_count = packed.shape[0] * 32
    shifts = jnp.arange(32, dtype=jnp.int32)
    bit_values = jnp.right_shift(packed[:, None, :], shifts[None, :, None]) & 1
    bit_values = bit_values.reshape(day_count, packed.shape[1]).T
    thirds = offsets % 3
    season_day = thirds[:, None] * day_count + jnp.arange(day_count, dtype=jnp.int32)[None, :]
    observed = jnp.where((bit_values == 1) & (season_day < CALENDAR), 1.0, 0.0).astype(jnp.float32)
    return (observed, thirds)


def exact_dot(left, right):
    return jnp.dot(left, right, precision=lax.Precision.HIGHEST, preferred_element_type=jnp.float32)


def per_device(temps, day_bits, block_offset, block_counts, station_cell):
    owners = lax.axis_size("sta")
    stations = station_cell.shape[0]
    block_total, day_count = temps.shape
    row_width = 3 * day_count
    cell_dev = CELLS // owners
    capacity = 4 * stations // owners
    slot_total = owners * capacity
    counts = block_counts[0].astype(jnp.float32)
    observed, thirds = observed_days(day_bits, block_offset)
    station_ids = jnp.arange(stations, dtype=jnp.int32)
    upper_ones = (station_ids[:, None] <= station_ids[None, :]).astype(jnp.float32)
    ends_at = exact_dot(counts[None, :], upper_ones)[0]
    block_rows = 512
    block_groups = block_total // block_rows
    row_blocks = (
        jnp.arange(block_total, dtype=jnp.int32)
        .reshape(block_groups, block_rows)
        .astype(jnp.float32)
    )
    third_blocks = thirds.reshape(block_groups, block_rows)

    def find_segment(inputs):
        row_block, third_block = inputs
        owning = jnp.sum((ends_at[None, :] <= row_block[:, None]).astype(jnp.int32), axis=1)
        return owning * 3 + third_block

    segment_blocks = lax.map(find_segment, (row_blocks, third_blocks))
    segment_ids = jnp.arange(stations * 3, dtype=jnp.int32)
    stacked = jnp.concatenate([observed * temps, observed], axis=1).reshape(
        block_groups, block_rows, 2 * day_count
    )

    def add_block(total, inputs):
        values, segment_block = inputs
        onehot = (segment_ids[:, None] == segment_block[None, :]).astype(jnp.float32)
        return (total + exact_dot(onehot, values), None)

    both_sums, unused = lax.scan(
        add_block, jnp.zeros((stations * 3, 2 * day_count), jnp.float32), (stacked, segment_blocks)
    )
    station_sums = both_sums[:, :day_count].reshape(stations, row_width)
    station_tallies = both_sums[:, day_count:].reshape(stations, row_width)
    owner_of = station_cell // cell_dev
    local_cell = station_cell - owner_of * cell_dev
    member = (owner_of[:, None] == jnp.arange(owners, dtype=jnp.int32)[None, :]).astype(jnp.float32)
    lower_strict = (station_ids[:, None] > station_ids[None, :]).astype(jnp.float32)
    before = exact_dot(lower_strict, member)
    slot_rank = jnp.sum(before * member, axis=1).astype(jnp.int32)
    slot_place = owner_of * capacity + slot_rank
    placing = (jnp.arange(slot_total, dtype=jnp.int32)[:, None] == slot_place[None, :]).astype(
        jnp.float32
    )
    station_both = jnp.concatenate(
        [station_sums, station_tallies, local_cell.astype(jnp.float32)[:, None]], axis=1
    )
    send_both = exact_dot(placing, station_both)
    send_sums = send_both[:, :row_width]
    send_tallies = send_both[:, row_width : 2 * row_width]
    send_cells = send_both[:, 2 * row_width]
    got_sums, got_tallies, got_cells = (
        lax.all_to_all(
            send_sums.reshape(owners, capacity, row_width),
            "sta",
            split_axis=0,
            concat_axis=0,
            tiled=True,
        ),
        lax.all_to_all(
            send_tallies.reshape(owners, capacity, row_width),
            "sta",
            split_axis=0,
            concat_axis=0,
            tiled=True,
        ),
        lax.all_to_all(
            send_cells.reshape(owners, capacity), "sta", split_axis=0, concat_axis=0, tiled=True
        ),
    )
    got_index = got_cells.reshape(-1).astype(jnp.int32)
    cell_onehot = (jnp.arange(cell_dev, dtype=jnp.int32)[:, None] == got_index[None, :]).astype(
        jnp.float32
    )
    cell_sums = exact_dot(cell_onehot, got_sums.reshape(-1, row_width))
    cell_tallies = exact_dot(cell_onehot, got_tallies.reshape(-1, row_width))
    cell_sums, cell_tallies = lax.psum((cell_sums, cell_tallies), "yr")
    climatology = cell_sums / jnp.maximum(cell_tallies, 1.0)
    outgoing = exact_dot(cell_onehot.T, climatology).reshape(owners, capacity, row_width)
    incoming = lax.all_to_all(outgoing, "sta", split_axis=0, concat_axis=0, tiled=True)
    station_clim = exact_dot(placing.T, incoming.reshape(-1, row_width))
    clim_rows = station_clim.reshape(stations * 3, day_count)

    def pull_block(segment_block):
        onehot = (segment_block[:, None] == segment_ids[None, :]).astype(jnp.float32)
        return exact_dot(onehot, clim_rows)

    block_clim = lax.map(pull_block, segment_blocks).reshape(block_total, day_count)
    anomalies = observed * (temps - block_clim)
    return (anomalies, climatology)


def solution(mesh):
    in_specs = (
        P(("sta", "yr"), None),
        P(None, ("sta", "yr")),
        P(("sta", "yr")),
        P("yr", "sta"),
        P("sta"),
    )
    out_specs = (P(("sta", "yr"), None), P("sta", None))
    return jax.shard_map(
        per_device, mesh=mesh, in_specs=in_specs, out_specs=out_specs, check_vma=False
    )
```

profile of v0, /device:TPU:0, one launch (start us, length us, event | category | flops | bytes accessed | tf_op | source)
XLA Modules:
  0.0 332.9 jit_solution(11253342683898192424)
XLA Ops:
  8.0 3.6 %copy.48 = f32[6144,128]{0,1:T(8,128)} copy(f32[6144,128]{1,0:T(8,128)} %param.11) | data formatting | bytes 6291456 | tf_op args[0]
  11.6 2.9 fusion.39
  14.5 3.1 pad_maximum_fusion
  17.6 6.6 %copy.41 = f32[6144,256]{1,0:T(8,128)} copy(f32[6144,256]{0,1:T(8,128)} %pad_maximum_fusion) | data formatting | bytes 12582912 | tf_op jit(solution)/shard_map/concatenate | solution.py:56
  24.3 4.4 %while.32 = (s32[]{:T(128)}, s32[12,512]{1,0:T(8,128)S(1)}, f32[1,256]{1,0:T(1,128)S(1)}, f32[12,512]{1,0:T(8,128)S(1)}, s32[12,512]{1,0:T(8,128)S(1)}, /*index=5*/s32[]{:T(128)}, s32[]{:T(128)}) while((s32[]{:T(128)}, s32[12,512]{1,0:T(8,128)S(1)}, f32[1,256]{1,0:T(1,128)S(1)}, f32[12,512]{1,0:T(8,128)S(1)}, s32[12,512]{1,0:T(8,128)S(1)}, ...), condition=%wide.region_2.3_spmd, body=%wide.region_0.2_spmd.sunk | while | flops 393730 | bytes 23641 | solution.py:54
  28.8 27.1 %while.34 = (s32[]{:T(128)}, f32[768,256]{1,0:T(8,128)S(1)}, s32[12,512]{1,0:T(8,128)S(1)}, f32[12,512,256]{2,1,0:T(8,128)}, s32[]{:T(128)}, /*index=5*/s32[]{:T(128)}) while((s32[]{:T(128)}, f32[768,256]{1,0:T(8,128)S(1)}, s32[12,512]{1,0:T(8,128)S(1)}, f32[12,512,256]{2,1,0:T(8,128)}, s32[]{:T(128)}, /*index=5*/s32[]{:T(128)}) %tuple.78), condition=%wide.region_5.6_spmd.clone, body=%wide.region_4.5_spmd.clone.sunk | while | flops 1208745984 | bytes 2103891 | solution.py:65
  28.8 2.2 fusion.53
  31.0 2.2 fusion.53
  33.3 2.2 fusion.53
  35.6 2.2 fusion.53
  37.8 2.2 fusion.53
  40.1 2.2 fusion.53
  42.3 2.2 fusion.53
  44.6 2.2 fusion.53
  46.9 2.2 fusion.53
  49.1 2.2 fusion.53
  51.4 2.2 fusion.53
  53.6 2.2 fusion.53
  58.0 2.6 fusion.26
  61.2 7.3 %all-to-all-start = ((f32[8,1,128]{2,1,0:T(1,128)}), f32[8,1,128]{2,1,0:T(1,128)S(1)}, u32[]{:S(2)}, u32[]{:S(2)}) async-start(f32[8,1,128]{2,1,0:T(1,128)} %slice_bitcast_fusion.2), calls=%async_computation | async-start | bytes 8192 | tf_op jit(solution)/shard_map/all_to_all | solution.py:102
  71.1 3.9 %all-to-all-done = f32[8,1,128]{2,1,0:T(1,128)S(1)} async-done(((f32[8,1,128]{2,1,0:T(1,128)}), f32[8,1,128]{2,1,0:T(1,128)S(1)}, u32[]{:S(2)}, u32[]{:S(2)}) %all-to-all-start) | async-done | bytes 4128 | tf_op jit(solution)/shard_map/all_to_all | solution.py:102
  75.0 3.6 %all-to-all-start.2 = ((f32[8,128,384]{1,2,0:T(8,128)}), f32[8,128,384]{1,2,0:T(8,128)S(1)}, u32[]{:S(2)}, u32[]{:S(2)}) async-start(f32[8,128,384]{1,2,0:T(8,128)} %bitcast.60), calls=%async_computation.2 | async-start | bytes 3145728 | tf_op jit(solution)/shard_map/all_to_all | solution.py:95
  79.8 34.7 %all-to-all-done.2 = f32[8,128,384]{1,2,0:T(8,128)S(1)} async-done(((f32[8,128,384]{1,2,0:T(8,128)}), f32[8,128,384]{1,2,0:T(8,128)S(1)}, u32[]{:S(2)}, u32[]{:S(2)}) %all-to-all-start.2) | async-done | bytes 1572896 | tf_op jit(solution)/shard_map/all_to_all | solution.py:95
  114.5 3.6 %all-to-all-start.1 = ((f32[8,128,384]{1,2,0:T(8,128)}), f32[8,128,384]{1,2,0:T(8,128)S(1)}, u32[]{:S(2)}, u32[]{:S(2)}) async-start(f32[8,128,384]{1,2,0:T(8,128)} %bitcast.61), calls=%async_computation.1 | async-start | bytes 3145728 | tf_op jit(solution)/shard_map/all_to_all | solution.py:88
  118.3 1.6 copy.47
  120.0 7.0 %fusion.15 = f32[1296,384]{1,0:T(8,128)} fusion(f32[1024,384]{1,0:T(8,128)} %bitcast.81, s32[1024]{0:T(1024)S(1)} %bitcast.89), kind=kOutput, calls=%fused_computation.23 | convolution fusion | flops 6116622336 | bytes 3567616 | tf_op jit(solution)/shard_map/dot_general | solution.py:24
  127.0 28.1 %all-to-all-done.1 = f32[8,128,384]{1,2,0:T(8,128)S(1)} async-done(((f32[8,128,384]{1,2,0:T(8,128)}), f32[8,128,384]{1,2,0:T(8,128)S(1)}, u32[]{:S(2)}, u32[]{:S(2)}) %all-to-all-start.1) | async-done | bytes 1572896 | tf_op jit(solution)/shard_map/all_to_all | solution.py:88
  155.6 5.6 %fusion.16 = f32[1296,384]{1,0:T(8,128)} fusion(f32[1024,384]{1,0:T(8,128)S(1)} %bitcast.82, s32[1024]{0:T(1024)S(1)} %bitcast.90), kind=kOutput, calls=%fused_computation.24 | convolution fusion | flops 6116622336 | bytes 3567616 | tf_op jit(solution)/shard_map/dot_general | solution.py:24
  161.2 81.4 %all-reduce.3.cloned.1.call-done = (f32[1296,384]{1,0:T(8,128)}, f32[1296,384]{1,0:T(8,128)}) async-done(((f32[1296,384]{1,0:T(8,128)}, f32[1296,384]{1,0:T(8,128)}), (f32[1296,384]{1,0:T(8,128)}, f32[1296,384]{1,0:T(8,128)})) %all-reduce.3.cloned.1.call-update) | async-done | bytes 3981328 | tf_op jit(solution)/shard_map/psum | solution.py:112
  242.6 2.4 maximum_divide_fusion
  245.1 6.4 %fusion.14 = f32[1024,384]{1,0:T(8,128)} fusion(f32[1296,384]{1,0:T(8,128)S(1)} %maximum_divide_fusion, s32[1024]{0:T(1024)S(1)} %bitcast.91), kind=kOutput, calls=%fused_computation.22 | convolution fusion | flops 6116622336 | bytes 3567616 | tf_op jit(solution)/shard_map/dot_general | solution.py:24
  251.5 5.5 %all-to-all-start.3 = ((f32[8,128,384]{2,1,0:T(8,128)}), f32[8,128,384]{2,1,0:T(8,128)S(1)}, u32[]{:S(2)}, u32[]{:S(2)}) async-start(f32[8,128,384]{2,1,0:T(8,128)} %bitcast.15), calls=%async_computation.3 | async-start | bytes 3145728 | tf_op jit(solution)/shard_map/all_to_all | solution.py:115
  257.0 36.8 %all-to-all-done.3 = f32[8,128,384]{2,1,0:T(8,128)S(1)} async-done(((f32[8,128,384]{2,1,0:T(8,128)}), f32[8,128,384]{2,1,0:T(8,128)S(1)}, u32[]{:S(2)}, u32[]{:S(2)}) %all-to-all-start.3) | async-done | bytes 1572896 | tf_op jit(solution)/shard_map/all_to_all | solution.py:115
  295.1 19.2 %while.33 = (s32[]{:T(128)}, f32[12,512,128]{2,1,0:T(8,128)}, s32[12,512]{1,0:T(8,128)S(1)}, f32[768,128]{1,0:T(8,128)S(1)}, s32[]{:T(128)}) while((s32[]{:T(128)}, f32[12,512,128]{2,1,0:T(8,128)}, s32[12,512]{1,0:T(8,128)S(1)}, f32[768,128]{1,0:T(8,128)S(1)}, s32[]{:T(128)}) %tuple.79), condition=%wide.region_9.10_spmd.clone, body=%wide.region_8.9_spmd.clone.sunk | while | flops 604372992 | bytes 662081 | solution.py:123
  295.1 1.6 fusion.51
  296.7 1.6 fusion.51
  298.3 1.6 fusion.51
  299.9 1.6 fusion.51
  301.4 1.6 fusion.51
  303.0 1.6 fusion.51
  306.2 1.6 fusion.51
  307.8 1.6 fusion.51
  309.4 1.6 fusion.51
  311.0 1.6 fusion.51
  312.6 1.6 fusion.51
  314.2 3.7 %copy.49 = f32[6144,128]{0,1:T(8,128)} copy(f32[6144,128]{1,0:T(8,128)} %bitcast.80) | data formatting | bytes 6291456 | tf_op jit(solution)/shard_map/reshape | solution.py:123
  317.9 4.6 %subtract_multiply_fusion = f32[6144,128]{0,1:T(8,128)} fusion(f32[6144,128]{0,1:T(8,128)S(1)} %copy-done, f32[6144,128]{0,1:T(8,128)} %copy.49, s32[6144]{0:T(1024)S(1)} %get-tuple-element.163, s32[128]{0:T(128)S(1)} %shift_right_arithmetic.23, s32[4,6144]{1,0:T(4,128)S(1)} %copy-done.3), kind=kLoop, calls=%fused_computation.28 | loop fusion | flops 7077888 | bytes 9560576 | tf_op jit(solution)/shard_map/mul | solution.py:124
  322.5 3.5 %copy.50 = f32[6144,128]{1,0:T(8,128)} copy(f32[6144,128]{0,1:T(8,128)} %subtract_multiply_fusion) | data formatting | bytes 6291456
  (123 shorter events, 15.2 us)
Async XLA Ops:
  8.0 3.7 %copy-start.3 = (s32[4,6144]{1,0:T(4,128)S(1)}, s32[4,6144]{1,0:T(4,128)}, u32[]{:S(2)}) copy-start(s32[4,6144]{1,0:T(4,128)} %param.12) | copy-start | bytes 294916
  17.6 6.6 %copy-start.5 = (s32[1,256]{1,0:T(1,128)S(1)}, s32[1,256]{1,0:T(1,128)}, u32[]{:S(2)}) copy-start(s32[1,256]{1,0:T(1,128)} %param.14) | copy-start | bytes 3076
  55.8 1.8 copy-start.4
  61.2 13.8 %all-to-all-start = ((f32[8,1,128]{2,1,0:T(1,128)}), f32[8,1,128]{2,1,0:T(1,128)S(1)}, u32[]{:S(2)}, u32[]{:S(2)}) async-start(f32[8,1,128]{2,1,0:T(1,128)} %slice_bitcast_fusion.2), calls=%async_computation | async-start | bytes 8192 | tf_op jit(solution)/shard_map/all_to_all | solution.py:102
  69.8 8.7 %copy-start.1 = (f32[48,8,8,128]{3,2,1,0:T(8,128)S(1)}, f32[48,8,8,128]{3,2,1,0:T(8,128)}, u32[]{:S(2)}) copy-start(f32[48,8,8,128]{3,2,1,0:T(8,128)} %get-tuple-element.158) | copy-start | bytes 4718596
  75.0 39.5 %all-to-all-start.2 = ((f32[8,128,384]{1,2,0:T(8,128)}), f32[8,128,384]{1,2,0:T(8,128)S(1)}, u32[]{:S(2)}, u32[]{:S(2)}) async-start(f32[8,128,384]{1,2,0:T(8,128)} %bitcast.60), calls=%async_computation.2 | async-start | bytes 3145728 | tf_op jit(solution)/shard_map/all_to_all | solution.py:95
  114.5 40.6 %all-to-all-start.1 = ((f32[8,128,384]{1,2,0:T(8,128)}), f32[8,128,384]{1,2,0:T(8,128)S(1)}, u32[]{:S(2)}, u32[]{:S(2)}) async-start(f32[8,128,384]{1,2,0:T(8,128)} %bitcast.61), calls=%async_computation.1 | async-start | bytes 3145728 | tf_op jit(solution)/shard_map/all_to_all | solution.py:88
  118.1 124.6 %all-reduce.3.cloned.1.call-start = ((), (), s32[]{:S(2)}) async-start(), calls=%async_computation.4 | async-start | bytes 7962624 | tf_op jit(solution)/shard_map/psum | solution.py:112
  245.1 6.5 %copy-start.2 = (f32[1296,384]{1,0:T(8,128)}, f32[1296,384]{1,0:T(8,128)S(1)}, u32[]{:S(2)}) copy-start(f32[1296,384]{1,0:T(8,128)S(1)} %maximum_divide_fusion) | copy-start | bytes 5971972
  251.5 42.3 %all-to-all-start.3 = ((f32[8,128,384]{2,1,0:T(8,128)}), f32[8,128,384]{2,1,0:T(8,128)S(1)}, u32[]{:S(2)}, u32[]{:S(2)}) async-start(f32[8,128,384]{2,1,0:T(8,128)} %bitcast.15), calls=%async_computation.3 | async-start | bytes 3145728 | tf_op jit(solution)/shard_map/all_to_all | solution.py:115
  314.2 3.7 %copy-start = (f32[6144,128]{0,1:T(8,128)S(1)}, f32[6144,128]{0,1:T(8,128)}, u32[]{:S(2)}) copy-start(f32[6144,128]{0,1:T(8,128)} %copy.48) | copy-start | bytes 9437188
Sparse Core Ops, SparseCore 0:
  161.3 81.2 all-reduce.2
where the time goes:
time: 334 us; the launch traced here: 333 us
  waiting for transfers between devices  185 us (55%)
  matrix products  68.8 us (21%)
  local copies, waits for them, and re-layouts  27.1 us (8%)
  starting transfers between devices  20.2 us (6%)
  other arithmetic  16.7 us (5%)
  between operations  14.2 us (4%)
    psum x1, waiting for transfers between devices, per_device(): cell_sums, cell_tallies = lax.psum((cell_sums, cell_tallies), 'yr')  81.4 us
    dot_general x31, matrix products, exact_dot(): jnp.dot(left, right, precision=lax.Precision.HIGHEST, preferred_element_t...  68.8 us
    all_to_all x1, waiting for transfers between devices, per_device(): lax.all_to_all(outgoing, 'sta', split_axis=0, concat_axis=0, tiled=True)  36.8 us
    all_to_all x1, waiting for transfers between devices, per_device(): lax.all_to_all(send_tallies.reshape(owners, capacity, row_width), 'sta',...  34.7 us
    all_to_all x1, waiting for transfers between devices, per_device(): lax.all_to_all(send_sums.reshape(owners, capacity, row_width), 'sta', spl...  28.1 us
    unnamed x15, local copies, waits for them, and re-layouts  8.51 us
    all_to_all x1, starting transfers between devices, per_device(): lax.all_to_all(send_cells.reshape(owners, capacity), 'sta', split_axis=0,...  7.31 us
  transfers between devices with their start and end apart: 5, of which 5 were waited for; matrix products, arithmetic and copies ran while one was open for 4% of the time, Pallas kernels for 0%

commit v1 on v0

v1 whole, which is shorter than its diff:
```python
import functools

import jax
import jax.numpy as jnp
from jax import lax
from jax.experimental import pallas as pl
from jax.experimental.pallas import tpu as pltpu
from jax.sharding import PartitionSpec as P

CELLS = 10368
CALENDAR = 365
MOST_BLOCKS = 48
LANES = 128
F32 = jnp.float32
BF16 = jnp.bfloat16


def round_up(value, step):
    return (value + step - 1) // step * step


def day_code(bits, offsets):
    rows = bits.shape[1]
    third = offsets - 3 * ((offsets * 21846) >> 16)
    words = jnp.concatenate(
        [jnp.broadcast_to(bits[w : w + 1], (32, rows)) for w in range(bits.shape[0])], axis=0
    )
    day = lax.broadcasted_iota(jnp.int32, words.shape, 0)
    bit = (words >> (day & 31)) & 1
    observed = jnp.where(third * LANES + day < CALENDAR, bit, 0)
    return third, (observed + 2 * third).astype(F32)


def split_two(value):
    high = value.astype(BF16)
    return high, (value - high.astype(F32)).astype(BF16)


def lane_group(rows, width):
    return lax.broadcasted_iota(jnp.int32, (rows, LANES), 1) // width


def gather_lanes(parts, shifts, width):
    group = lane_group(parts[0].shape[0], width)
    total = None
    for j, (part, shift) in enumerate(zip(parts, shifts)):
        shift = shift % LANES
        moved = pltpu.roll(part, shift, 1) if shift else part
        total = jnp.where(group == j, moved, 0.0 if total is None else total)
    return total


def sums_kernel(ranges, packed, temps_ref, bits_ref, offs_ref, counts_ref, out_ref, acc, edges):
    step = pl.program_id(0)
    rows = temps_ref.shape[0]
    stations = counts_ref.shape[1]

    @pl.when(step == 0)
    def _():
        acc[...] = jnp.zeros_like(acc)
        counts = jnp.broadcast_to(counts_ref[...].astype(F32), (stations, stations))
        at = lax.broadcasted_iota(jnp.int32, (stations, stations), 0)
        of = lax.broadcasted_iota(jnp.int32, (stations, stations), 1)
        ends = jnp.sum(jnp.where(of <= at, counts, 0.0), axis=1, keepdims=True)
        starts = jnp.sum(jnp.where(of < at, counts, 0.0), axis=1, keepdims=True)
        edges[0] = jnp.broadcast_to(starts, (stations, LANES)).astype(jnp.int32)
        edges[1] = jnp.broadcast_to(ends, (stations, LANES)).astype(jnp.int32)

    third, code = day_code(bits_ref[...], offs_ref[...])
    code = code.T
    observed = code - 2.0 * jnp.floor(code * 0.5)
    high, low = split_two(temps_ref[...] * observed)
    values = jnp.concatenate([high, low, observed.astype(BF16)], axis=1)
    row = lax.broadcasted_iota(jnp.int32, (1, rows), 1) + step * rows
    inside = (row >= edges[0][:, 0:1]) & (row < edges[1][:, 0:1])
    station_third = jnp.where(inside, third, 3)
    onehot = jnp.concatenate(
        [jnp.where(station_third == k, 1.0, 0.0).astype(BF16) for k in range(3)], axis=0
    )
    acc[...] += jnp.dot(onehot, values, preferred_element_type=F32)

    @pl.when(step == pl.num_programs(0) - 1)
    def _():
        width = LANES // ranges
        third_of = [acc[k * stations : (k + 1) * stations, :] for k in range(3)]
        groups = [t[:, :LANES] + t[:, LANES : 2 * LANES] for t in third_of]
        tallies = [t[:, 2 * LANES :] for t in third_of]
        if packed:
            groups.append(tallies[0] + 256.0 * tallies[1] + 65536.0 * tallies[2])
        else:
            groups.extend(tallies)
        for r in range(ranges):
            out_ref[r] = gather_lanes(groups, [width * (k - r) for k in range(len(groups))], width)


def cells_kernel(ranges, packed, cell_dev, cell_pad, got_ref, first_ref, own_ref, out_ref, acc):
    shards, _, _ = got_ref.shape
    stations = own_ref.shape[0]
    width = LANES // ranges
    ids = lax.broadcasted_iota(jnp.int32, (cell_pad, 1), 0).astype(F32) + first_ref[0, 0].astype(F32)
    acc[...] = jnp.zeros_like(acc)
    group = lane_group(stations, width)
    for s in range(shards):
        both = got_ref[s, :stations, :]
        high, low = split_two(both)
        if packed:
            tally = both.astype(jnp.int32)
            tally = jnp.where(
                group == 0,
                pltpu.roll(tally, LANES - 3 * width, 1) & 255,
                jnp.where(
                    group == 1,
                    (pltpu.roll(tally, LANES - 2 * width, 1) >> 8) & 255,
                    (pltpu.roll(tally, LANES - width, 1) >> 16) & 255,
                ),
            ).astype(F32)
            values = [high, low, tally.astype(BF16)]
        else:
            tally = pltpu.roll(both, LANES - 3 * width, 1)
            values = [high, low, *split_two(tally)]
        values = jnp.concatenate(values, axis=1)
        for q in range(stations // LANES):
            cells = got_ref[s, stations + q : stations + q + 1, :]
            part = values[q * LANES : (q + 1) * LANES]
            hot = jnp.where(ids == cells, 1.0, 0.0).astype(BF16)
            acc[:cell_pad] += jnp.dot(hot, part, preferred_element_type=F32)
            hot = jnp.where(own_ref[...] == cells, 1.0, 0.0).astype(BF16)
            acc[cell_pad:] += jnp.dot(hot, part, preferred_element_type=F32)
    tallies = acc[:, 2 * LANES : 3 * LANES]
    if not packed:
        tallies = tallies + acc[:, 3 * LANES :]
    acc[:, :LANES] = (acc[:, :LANES] + acc[:, LANES : 2 * LANES]) / jnp.maximum(tallies, 1.0)
    cell_rows, station_rows = cell_pad // ranges, stations // ranges
    for k in range(3):
        shifts = [width * (j - k) for j in range(ranges)]
        out_ref[k, :cell_rows] = gather_lanes(
            [acc[j * cell_rows : (j + 1) * cell_rows, :LANES] for j in range(ranges)], shifts, width
        )
        first = [cell_pad + j * station_rows for j in range(ranges)]
        out_ref[k, cell_rows:] = gather_lanes(
            [acc[f : f + station_rows, :LANES] for f in first], shifts, width
        )


def unpack(clim_ref, k, j, first, count, ranges, width):
    return gather_lanes(
        [clim_ref[r, k, first : first + count, :] for r in range(ranges)],
        [width * (r - j) for r in range(ranges)],
        width,
    )


def anomaly_kernel(
    ranges, cell_dev, cell_pad, temps_ref, bits_ref, offs_ref, counts_ref, clim_ref,
    out_ref, climatology_ref, edges, table,
):
    step = pl.program_id(0)
    rows = temps_ref.shape[0]
    stations = counts_ref.shape[1]
    width = LANES // ranges
    cell_rows, station_rows = cell_pad // ranges, stations // ranges

    @pl.when(step == 0)
    def _():
        at = lax.broadcasted_iota(jnp.int32, (stations, stations), 0)
        of = lax.broadcasted_iota(jnp.int32, (stations, stations), 1)
        counts = jnp.broadcast_to(counts_ref[...].astype(F32), (stations, stations))
        column = jnp.sum(jnp.where(at == of, counts, 0.0), axis=1, keepdims=True)
        ends = jnp.sum(jnp.where(at <= of, column, 0.0), axis=0, keepdims=True)
        edges[0:1] = (ends - counts_ref[...].astype(F32)).astype(jnp.int32)
        edges[1:2] = ends.astype(jnp.int32)
        for k in range(3):
            for j in range(ranges):
                part = unpack(clim_ref, k, j, cell_rows, station_rows, ranges, width)
                high, low = split_two(part)
                at_rows = slice(j * station_rows, (j + 1) * station_rows)
                table[at_rows, 2 * k * LANES : (2 * k + 1) * LANES] = high
                table[at_rows, (2 * k + 1) * LANES : (2 * k + 2) * LANES] = low
                count = min(cell_dev - j * cell_rows, cell_rows)
                if count > 0:
                    climatology_ref[
                        j * cell_rows : j * cell_rows + count, k * LANES : (k + 1) * LANES
                    ] = unpack(clim_ref, k, j, 0, count, ranges, width)

    _, code = day_code(bits_ref[...], offs_ref[...])
    code = code.T
    third = jnp.floor(code * 0.5)
    row = lax.broadcasted_iota(jnp.int32, (rows, stations), 0) + step * rows
    inside = (row >= edges[0:1]) & (row < edges[1:2])
    onehot = jnp.where(inside, 1.0, 0.0).astype(BF16)
    found = jnp.dot(onehot, table[...], preferred_element_type=F32)
    clim = [
        found[:, 2 * k * LANES : (2 * k + 1) * LANES]
        + found[:, (2 * k + 1) * LANES : (2 * k + 2) * LANES]
        for k in range(3)
    ]
    block_clim = jnp.where(third == 0.0, clim[0], jnp.where(third == 1.0, clim[1], clim[2]))
    out_ref[...] = (code - 2.0 * third) * (temps_ref[...] - block_clim)


def exchange_in(sums, cells, owners, ranges):
    mine = lax.psum_scatter(sums, "yr", scatter_dimension=0, tiled=False)
    return lax.all_gather(jnp.concatenate([mine, cells], axis=0), "sta")


def exchange_out(part, ranges):
    return lax.all_gather(part, "yr")


def per_device(temps, day_bits, block_offset, block_counts, station_cell):
    owners, ranges = lax.axis_size("sta"), lax.axis_size("yr")
    stations = station_cell.shape[0]
    block_total, day_count = temps.shape
    cell_dev = CELLS // owners
    cell_pad = round_up(cell_dev, 8 * ranges)
    packed = ranges * MOST_BLOCKS < 256
    rows = 1024 if block_total % 1024 == 0 else block_total
    offsets = block_offset.reshape(1, block_total)
    row_specs = [
        pl.BlockSpec((rows, day_count), lambda i: (i, 0)),
        pl.BlockSpec((day_bits.shape[0], rows), lambda i: (0, i)),
        pl.BlockSpec((1, rows), lambda i: (0, i)),
        pl.BlockSpec((1, stations), lambda i: (0, 0)),
    ]
    params = pltpu.CompilerParams(
        dimension_semantics=("arbitrary",), vmem_limit_bytes=48 * 1024 * 1024
    )
    sums = pl.pallas_call(
        functools.partial(sums_kernel, ranges, packed),
        grid=(block_total // rows,),
        in_specs=row_specs,
        out_specs=pl.BlockSpec((ranges, stations, LANES), lambda i: (0, 0, 0)),
        out_shape=jax.ShapeDtypeStruct((ranges, stations, LANES), F32),
        scratch_shapes=[
            pltpu.VMEM((3 * stations, 3 * LANES), F32),
            pltpu.VMEM((2, stations, LANES), jnp.int32),
        ],
        compiler_params=params,
    )(temps, day_bits, offsets, block_counts)

    cell_row_count = round_up(stations // LANES, 8)
    cell_rows = jnp.pad(
        station_cell.astype(F32).reshape(stations // LANES, LANES),
        ((0, cell_row_count - stations // LANES), (0, 0)),
    )
    got = exchange_in(sums, cell_rows, owners, ranges)

    first = (lax.axis_index("sta") * cell_dev).astype(jnp.int32).reshape(1, 1)
    part_rows = (cell_pad + stations) // ranges
    part = pl.pallas_call(
        functools.partial(cells_kernel, ranges, packed, cell_dev, cell_pad),
        in_specs=[
            pl.BlockSpec(memory_space=pltpu.VMEM),
            pl.BlockSpec(memory_space=pltpu.SMEM),
            pl.BlockSpec(memory_space=pltpu.VMEM),
        ],
        out_specs=pl.BlockSpec(memory_space=pltpu.VMEM),
        out_shape=jax.ShapeDtypeStruct((3, part_rows, LANES), F32),
        scratch_shapes=[pltpu.VMEM((cell_pad + stations, (3 if packed else 4) * LANES), F32)],
        compiler_params=pltpu.CompilerParams(vmem_limit_bytes=48 * 1024 * 1024),
    )(got, first, station_cell.astype(F32).reshape(stations, 1))

    parts = exchange_out(part, ranges)

    return pl.pallas_call(
        functools.partial(anomaly_kernel, ranges, cell_dev, cell_pad),
        grid=(block_total // rows,),
        in_specs=row_specs
        + [pl.BlockSpec((ranges, 3, part_rows, LANES), lambda i: (0, 0, 0, 0))],
        out_specs=[
            pl.BlockSpec((rows, day_count), lambda i: (i, 0)),
            pl.BlockSpec((cell_dev, 3 * LANES), lambda i: (0, 0)),
        ],
        out_shape=[
            jax.ShapeDtypeStruct((block_total, day_count), F32),
            jax.ShapeDtypeStruct((cell_dev, 3 * LANES), F32),
        ],
        scratch_shapes=[
            pltpu.VMEM((8, stations), jnp.int32),
            pltpu.VMEM((stations, 6 * LANES), BF16),
        ],
        compiler_params=params,
    )(temps, day_bits, offsets, block_counts, parts)


def solution(mesh):
    in_specs = (
        P(("sta", "yr"), None),
        P(None, ("sta", "yr")),
        P(("sta", "yr")),
        P("yr", "sta"),
        P("sta"),
    )
    out_specs = (P(("sta", "yr"), None), P("sta", None))

    def run(*args):
        return tuple(per_device(*args))

    return jax.shard_map(
        run, mesh=mesh, in_specs=in_specs, out_specs=out_specs, check_vma=False
    )
```

time: 334 us -> 134 us (0.40)
  waiting for transfers between devices: 185 us -> 89.2 us
  matrix products: 68.8 us -> 0 us
  Pallas kernels: 0 us -> 20.5 us
  starting transfers between devices: 20.2 us -> 0.12 us
  local copies, waits for them, and re-layouts: 27.1 us -> 8.85 us
  other arithmetic: 16.7 us -> 1.57 us
    all_to_all x4 -> x0, waiting for transfers between devices: 103 us -> none  [the longest x1 36.8 us: per_device(): lax.all_to_all(outgoing, 'sta', split_axis=0, concat_axis=0, tiled=True)]
    psum x1 -> x0, waiting for transfers between devices: 81.4 us -> none  [per_device(): cell_sums, cell_tallies = lax.psum((cell_sums, cell_tallies), 'yr')]
    dot_general x31 -> x0, matrix products: 68.8 us -> none  [exact_dot(): jnp.dot(left, right, precision=lax.Precision.HIGHEST, preferred_element_t...]
    all_gather x0 -> x2, waiting for transfers between devices: none -> 64.7 us  [the longest x1 41.5 us: exchange_in(): return lax.all_gather(jnp.concatenate([mine, cells], axis=0), 'sta')]
    reduce_scatter x0 -> x1, waiting for transfers between devices: none -> 24.4 us  [exchange_in(): mine = lax.psum_scatter(sums, 'yr', scatter_dimension=0, tiled=False)]
    pallas_call x0 -> x3, Pallas kernels: none -> 20.5 us  [the longest x1 7.75 us: per_device(): pl.pallas_call(functools.partial(anomaly_kernel, ranges, cell_dev, cell_p...]
    all_to_all x4 -> x0, starting transfers between devices: 20 us -> none  [the longest x1 7.31 us: per_device(): lax.all_to_all(send_cells.reshape(owners, capacity), 'sta', split_axis=0,...]
    mul x15 -> x0, other arithmetic: 8.29 us -> none  [the longest x1 4.6 us: per_device(): anomalies = observed * (temps - block_clim)]
  transfers between devices with their start and end apart: 5 -> 3, of which waited for: 5 -> 3; matrix products, arithmetic and copies ran while one was open for 4% -> 0% of each run, Pallas kernels for 0% -> 0%
where the time goes in v1:
time: 134 us
  waiting for transfers between devices  89.2 us (67%)
  Pallas kernels  20.5 us (15%)
  between operations  13.8 us (10%)
  local copies, waits for them, and re-layouts  8.85 us (7%)
  other arithmetic  1.57 us (1%)
    all_gather x1, waiting for transfers between devices, exchange_in(): return lax.all_gather(jnp.concatenate([mine, cells], axis=0), 'sta')  41.5 us
    reduce_scatter x1, waiting for transfers between devices, exchange_in(): mine = lax.psum_scatter(sums, 'yr', scatter_dimension=0, tiled=False)  24.4 us
    all_gather x1, waiting for transfers between devices, exchange_out(): return lax.all_gather(part, 'yr')  23.2 us
    unnamed x26, local copies, waits for them, and re-layouts  8.72 us
    pallas_call x1, Pallas kernels, per_device(): pl.pallas_call(functools.partial(anomaly_kernel, ranges, cell_dev, cell_p...  7.75 us
    pallas_call x1, Pallas kernels, per_device(): pl.pallas_call(functools.partial(sums_kernel, ranges, packed), grid=(bloc...  7.32 us
    pallas_call x1, Pallas kernels, per_device(): pl.pallas_call(functools.partial(cells_kernel, ranges, packed, cell_dev,...  5.44 us
  transfers between devices with their start and end apart: 3, of which 3 were waited for; matrix products, arithmetic and copies ran while one was open for 0% of the time, Pallas kernels for 0%

profile of v1, /device:TPU:0, one launch (start us, length us, event | category | flops | bytes accessed | tf_op | source)
XLA Modules:
  0.0 134.1 jit_solution(17938235001873876065)
XLA Ops:
  7.2 0.0 copy-start.12
  7.2 0.0 reduce-scatter.2.cloned.1.call-start
  7.2 0.0 copy-start
  7.2 1.9 %copy-done = f32[6144,128]{1,0:T(8,128)S(1)} copy-done((f32[6144,128]{1,0:T(8,128)S(1)}, f32[6144,128]{1,0:T(8,128)}, u32[]{:S(2)}) %copy-start) | copy-done | bytes 3145752
  9.1 0.0 copy-start.6
  9.1 0.9 copy-done.6
  10.0 0.0 copy-start.8
  10.0 0.7 copy-done.8
  10.7 0.0 copy-start.10
  10.7 0.7 copy-done.10
  11.4 0.0 copy-start.7
  11.4 0.0 copy-start.9
  11.4 0.0 copy-start.11
  11.4 7.3 %shard_map.68 = f32[4,256,128]{2,1,0:T(8,128)S(1)} custom-call(f32[6144,128]{1,0:T(8,128)S(1)} %copy-done, s32[4,6144]{1,0:T(4,128)S(1)} %copy-done.6, s32[1,6144]{1,0:T(1,128)S(1)} %bitcast.10, s32[1,256]{1,0:T(1,128)S(1)} %copy-done.10), custom_call_target="tpu_custom_call" | custom-call | tf_op jit(solution)/shard_map/pallas_call | solution.py:228
  18.8 0.0 copy-start.4
  18.8 0.8 copy-done.4
  19.6 0.0 copy-start.1
  19.6 0.0 reduce-scatter.2.cloned.1.call-update
  19.6 0.0 all-gather.5.cloned.1.call-start
  19.6 0.0 copy-done.12
  19.7 24.4 %reduce-scatter.2.cloned.1.call-done = f32[1,256,128]{2,1,0:T(8,128)} async-done(((f32[4,256,128]{2,1,0:T(8,128)}), f32[1,256,128]{2,1,0:T(8,128)}) %reduce-scatter.2.cloned.1.call-update) | async-done | bytes 131088 | tf_op jit(solution)/shard_map/reduce_scatter | solution.py:202
  44.1 1.6 %select_maximum_fusion = f32[264,128]{1,0:T(8,128)} fusion(f32[2,128]{1,0:T(2,128)S(1)} %get-tuple-element.3, f32[256,128]{1,0:T(8,128)} %bitcast.12), kind=kLoop, calls=%fused_computation | loop fusion | flops 101376 | bytes 267264 | tf_op jit(solution)/shard_map/concatenate | solution.py:203
  45.7 0.0 all-gather.5.cloned.1.call-update
  45.7 0.0 all-gather.7.cloned.1.call-start
  45.7 0.1 copy.8.own_ref
  45.9 41.5 %all-gather.5.cloned.1.call-done = f32[2112,128]{1,0:T(8,128)} async-done(((f32[264,128]{1,0:T(8,128)}), f32[2112,128]{1,0:T(8,128)}) %all-gather.5.cloned.1.call-update) | async-done | bytes 1081360 | tf_op jit(solution)/shard_map/all_gather | solution.py:203
  87.4 0.0 copy-start.5
  87.4 1.2 copy-done.5
  88.6 5.4 %shard_map.69 = f32[3,392,128]{2,1,0:T(8,128)S(1)} custom-call(f32[8,264,128]{2,1,0:T(8,128)S(1)} %bitcast.9, s32[1,1]{1,0:T(1,128)} %bitcast.4.first_ref, f32[256,1]{1,0:T(8,128)S(1)} %copy.8.own_ref), custom_call_target="tpu_custom_call" | custom-call | tf_op jit(solution)/shard_map/pallas_call | solution.py:250
  94.1 0.0 copy-start.3
  94.1 0.8 copy-done.3
  94.9 0.0 all-gather.7.cloned.1.call-update
  94.9 23.2 %all-gather.7.cloned.1.call-done = f32[12,392,128]{2,1,0:T(8,128)} async-done(((f32[3,392,128]{2,1,0:T(8,128)}), f32[12,392,128]{2,1,0:T(8,128)}) %all-gather.7.cloned.1.call-update) | async-done | bytes 2408464 | tf_op jit(solution)/shard_map/all_gather | solution.py:207
  118.1 0.0 copy-done.7
  118.1 0.0 copy-done.9
  118.1 0.0 copy-done.11
  118.1 0.0 copy-done.1
  118.1 0.0 copy-start.2
  118.1 1.7 %copy-done.2 = f32[12,392,128]{2,1,0:T(8,128)S(1)} copy-done((f32[12,392,128]{2,1,0:T(8,128)S(1)}, f32[12,392,128]{2,1,0:T(8,128)}, u32[]{:S(2)}) %copy-start.2) | copy-done | bytes 2408472
  119.8 7.7 %shard_map.70 = (f32[6144,128]{1,0:T(8,128)}, f32[1296,384]{1,0:T(8,128)}) custom-call(f32[6144,128]{1,0:T(8,128)S(1)} %copy-done.1, s32[4,6144]{1,0:T(4,128)S(1)} %copy-done.7, s32[1,6144]{1,0:T(1,128)S(1)} %bitcast.11, s32[1,256]{1,0:T(1,128)S(1)} %copy-done.11, f32[4,3,392,128]{3,2,1,0:T(8,128)S(1)} %bitcast.8), custom_call_target="tpu_custom_call" | custom-call | tf_op jit(solution)/shard_map/pallas_call | solution.py:265
  (1 shorter events, 0.0 us)
Async XLA Ops:
  7.2 12.5 %copy-start.12 = (s32[256]{0:T(256)S(1)}, s32[256]{0:T(256)}, u32[]{:S(2)}) copy-start(s32[256]{0:T(256)} %param.9) | copy-start | bytes 3076
  7.2 36.9 %reduce-scatter.2.cloned.1.call-start = ((), (), s32[]{:S(2)}) async-start(), calls=%async_computation.1 | async-start | bytes 655360 | tf_op jit(solution)/shard_map/reduce_scatter | solution.py:202
  7.2 1.9 %copy-start = (f32[6144,128]{1,0:T(8,128)S(1)}, f32[6144,128]{1,0:T(8,128)}, u32[]{:S(2)}) copy-start(f32[6144,128]{1,0:T(8,128)} %temps_ref.3) | copy-start | bytes 9437188
  9.1 0.9 copy-start.6
  10.0 0.7 copy-start.8
  10.7 0.7 copy-start.10
  11.4 106.7 %copy-start.7 = (s32[4,6144]{1,0:T(4,128)S(1)}, s32[4,6144]{1,0:T(4,128)}, u32[]{:S(2)}) copy-start(s32[4,6144]{1,0:T(4,128)} %bits_ref.3) | copy-start | bytes 294916
  11.4 106.7 %copy-start.9 = (s32[6144]{0:T(1024)S(1)}, s32[6144]{0:T(1024)}, u32[]{:S(2)}) copy-start(s32[6144]{0:T(1024)} %param.7) | copy-start | bytes 73732
  11.4 106.7 %copy-start.11 = (s32[1,256]{1,0:T(1,128)S(1)}, s32[1,256]{1,0:T(1,128)}, u32[]{:S(2)}) copy-start(s32[1,256]{1,0:T(1,128)} %counts_ref.3) | copy-start | bytes 3076
  18.8 0.8 copy-start.4
  19.6 98.5 %copy-start.1 = (f32[6144,128]{1,0:T(8,128)S(1)}, f32[6144,128]{1,0:T(8,128)}, u32[]{:S(2)}) copy-start(f32[6144,128]{1,0:T(8,128)} %temps_ref.3) | copy-start | bytes 9437188
  19.6 67.8 %all-gather.5.cloned.1.call-start = ((), (), s32[]{:S(2)}) async-start(), calls=%async_computation.2 | async-start | bytes 1216512 | tf_op jit(solution)/shard_map/all_gather | solution.py:203
  45.7 72.4 %all-gather.7.cloned.1.call-start = ((), (), s32[]{:S(2)}) async-start(), calls=%async_computation.3 | async-start | bytes 3010560 | tf_op jit(solution)/shard_map/all_gather | solution.py:207
  87.4 1.2 copy-start.5
  94.1 0.8 copy-start.3
  118.1 1.7 %copy-start.2 = (f32[12,392,128]{2,1,0:T(8,128)S(1)}, f32[12,392,128]{2,1,0:T(8,128)}, u32[]{:S(2)}) copy-start(f32[12,392,128]{2,1,0:T(8,128)} %all-gather.7.cloned.1.call-done) | copy-start | bytes 7225348
Sparse Core Ops, SparseCore 0:
  19.7 24.3 reduce-scatter.1
  46.8 40.5 all-gather.4
  95.0 23.0 all-gather.6

commit v2 on v1

--- a/solution.py
+++ b/solution.py
@@ -198,13 +198,173 @@
     out_ref[...] = (code - 2.0 * third) * (temps_ref[...] - block_clim)
 
 
+def remote(src, dst, send, recv, where):
+    return pltpu.make_async_remote_copy(
+        src_ref=src, dst_ref=dst, send_sem=send, recv_sem=recv,
+        device_id=where, device_id_type=pl.DeviceIdType.MESH,
+    )
+
+
+def greet(peers):
+    barrier = pltpu.get_barrier_semaphore()
+    for where in peers:
+        pl.semaphore_signal(barrier, inc=1, device_id=where, device_id_type=pl.DeviceIdType.MESH)
+    pl.semaphore_wait(barrier, len(peers))
+
+
+def gather_kernel(
+    owners, ranges, major, sums_ref, cells_ref, out_ref, pair, partial, across,
+    pair_send, pair_recv, across_send, across_recv, far_send, far_recv, near_send, near_recv,
+):
+    stations = sums_ref.shape[1]
+    chips, minor = ranges // 2, owners // major
+    sta, yr = lax.axis_index("sta"), lax.axis_index("yr")
+    chip, core = yr // 2, lax.rem(yr, 2)
+    row, place = sta // minor, lax.rem(sta, minor)
+    partner = {"yr": chip * 2 + 1 - core}
+    chip_at = [lax.rem(chip + k, chips) for k in range(chips)]
+    chip_from = [lax.rem(chip + chips - k, chips) for k in range(chips)]
+    row_at = [lax.rem(row + k, major) for k in range(major)]
+    row_from = [lax.rem(row + major - k, major) for k in range(major)]
+    far = [{"sta": row_at[k] * minor + place} for k in range(1, major)]
+    near = [{"sta": row * minor + lax.rem(place + j, minor)} for j in range(1, minor)]
+    greet([partner] + [{"yr": c * 2 + core} for c in chip_at[1:]] + far + near)
+
+    pairs = []
+    for k in [*range(1, chips), 0]:
+        copy = remote(
+            sums_ref.at[chip_at[k] * 2 + 1 - core], pair.at[k],
+            pair_send.at[k], pair_recv.at[k], partner,
+        )
+        copy.start()
+        pairs.append(copy)
+    crossing = []
+    for k in range(1, chips):
+        pairs[k - 1].wait_recv()
+        partial[k - 1] = sums_ref[chip_at[k] * 2 + core] + pair[k]
+        copy = remote(
+            partial.at[k - 1], across.at[k - 1], across_send.at[k - 1], across_recv.at[k - 1],
+            {"yr": chip_at[k] * 2 + core},
+        )
+        copy.start()
+        crossing.append(copy)
+    pairs[-1].wait_recv()
+    total = sums_ref[yr] + pair[0]
+    for k, copy in enumerate(crossing):
+        copy.wait_recv()
+        total = total + across[k]
+    out_ref[sta, :stations] = total
+    out_ref[sta, stations:] = cells_ref[...]
+
+    sent = pairs + crossing
+    fars, nears = [], []
+    for k in range(1, major):
+        copy = remote(
+            out_ref.at[sta], out_ref.at[sta], far_send.at[k - 1], far_recv.at[k - 1], far[k - 1]
+        )
+        copy.start()
+        fars.append(copy)
+    for k in range(major):
+        if k:
+            fars[k - 1].wait_recv()
+        block = row_from[k] * minor + place
+        for j in range(1, minor):
+            at = k * max(minor - 1, 1) + j - 1
+            copy = remote(
+                out_ref.at[block], out_ref.at[block], near_send.at[at], near_recv.at[at],
+                near[j - 1],
+            )
+            copy.start()
+            nears.append(copy)
+    for copy in nears:
+        copy.wait_recv()
+    for copy in sent + fars + nears:
+        copy.wait_send()
+
+
 def exchange_in(sums, cells, owners, ranges):
-    mine = lax.psum_scatter(sums, "yr", scatter_dimension=0, tiled=False)
-    return lax.all_gather(jnp.concatenate([mine, cells], axis=0), "sta")
+    stations = sums.shape[1]
+    major = 4 if owners % 4 == 0 else owners
+    chips, minor = ranges // 2, owners // major
+    block = stations + cells.shape[0]
+    dma = pltpu.SemaphoreType.DMA
+    near_count = max(major * (minor - 1), 1)
+    crossings = max(chips - 1, 1)
+    return pl.pallas_call(
+        functools.partial(gather_kernel, owners, ranges, major),
+        in_specs=[pl.BlockSpec(memory_space=pltpu.VMEM)] * 2,
+        out_specs=pl.BlockSpec(memory_space=pltpu.VMEM),
+        out_shape=jax.ShapeDtypeStruct((owners, block, LANES), F32),
+        scratch_shapes=[
+            pltpu.VMEM((chips, stations, LANES), F32),
+            pltpu.VMEM((crossings, stations, LANES), F32),
+            pltpu.VMEM((crossings, stations, LANES), F32),
+            dma((chips,)), dma((chips,)), dma((crossings,)), dma((crossings,)),
+            dma((max(major - 1, 1),)), dma((max(major - 1, 1),)), dma((near_count,)), dma((near_count,)),
+        ],
+        compiler_params=pltpu.CompilerParams(
+            collective_id=0, has_side_effects=True, vmem_limit_bytes=48 * 1024 * 1024
+        ),
+    )(sums, cells)
+
+
+def spread_kernel(ranges, part_ref, out_ref, far_send, far_recv, near_send, near_recv):
+    chips = ranges // 2
+    chunks = part_ref.shape[0]
+    yr = lax.axis_index("yr")
+    chip, core = yr // 2, lax.rem(yr, 2)
+    partner = {"yr": chip * 2 + 1 - core}
+    others = [lax.rem(chip + k, chips) * 2 + core for k in range(1, chips)]
+    origins = [lax.rem(chip + chips - k, chips) * 2 + core for k in range(1, chips)]
+    greet([partner] + [{"yr": other} for other in others])
+    fars, nears = [], []
+    for t in range(chunks):
+        for k, other in enumerate(others):
+            at = t * len(others) + k
+            copy = remote(
+                part_ref.at[t], out_ref.at[yr, t], far_send.at[at], far_recv.at[at], {"yr": other}
+            )
+            copy.start()
+            fars.append(copy)
+    for t in range(chunks):
+        copy = remote(part_ref.at[t], out_ref.at[yr, t], near_send.at[t], near_recv.at[t], partner)
+        copy.start()
+        nears.append(copy)
+    out_ref[yr] = part_ref[...]
+    for t in range(chunks):
+        for k, origin in enumerate(origins):
+            at = t * len(others) + k
+            fars[at].wait_recv()
+            at = chunks + at
+            copy = remote(
+                out_ref.at[origin, t], out_ref.at[origin, t], near_send.at[at], near_recv.at[at],
+                partner,
+            )
+            copy.start()
+            nears.append(copy)
+    for copy in nears:
+        copy.wait_recv()
+    for copy in fars + nears:
+        copy.wait_send()
 
 
 def exchange_out(part, ranges):
-    return lax.all_gather(part, "yr")
+    chunks = part.shape[0]
+    crossings = chunks * (ranges // 2 - 1)
+    dma = pltpu.SemaphoreType.DMA
+    return pl.pallas_call(
+        functools.partial(spread_kernel, ranges),
+        in_specs=[pl.BlockSpec(memory_space=pltpu.VMEM)],
+        out_specs=pl.BlockSpec(memory_space=pltpu.VMEM),
+        out_shape=jax.ShapeDtypeStruct((ranges, *part.shape), F32),
+        scratch_shapes=[
+            dma((max(crossings, 1),)), dma((max(crossings, 1),)),
+            dma((chunks + crossings,)), dma((chunks + crossings,)),
+        ],
+        compiler_params=pltpu.CompilerParams(
+            collective_id=1, has_side_effects=True, vmem_limit_bytes=48 * 1024 * 1024
+        ),
+    )(part)
 
 
 def per_device(temps, day_bits, block_offset, block_counts, station_cell):

time: 134 us -> 72.6 us (0.54)
  waiting for transfers between devices: 89.2 us -> 0 us
  Pallas kernels: 20.5 us -> 65.9 us
  between operations: 13.8 us -> 0.7 us
  local copies, waits for them, and re-layouts: 8.85 us -> 4.34 us
    all_gather x2 -> x0, waiting for transfers between devices: 64.7 us -> none  [the longest x1 41.5 us: exchange_in(): return lax.all_gather(jnp.concatenate([mine, cells], axis=0), 'sta')]
    pallas_call x0 -> x2, Pallas kernels: none -> 45.3 us  [the longest x1 29.4 us: exchange_in(): pl.pallas_call(functools.partial(gather_kernel, owners, ranges, major), i...]
    reduce_scatter x1 -> x0, waiting for transfers between devices: 24.4 us -> none  [exchange_in(): mine = lax.psum_scatter(sums, 'yr', scatter_dimension=0, tiled=False)]
    unnamed x26 -> x10, local copies, waits for them, and re-layouts: 8.72 us -> 4.2 us
    concatenate x1 -> x0, other arithmetic: 1.57 us -> none  [exchange_in(): return lax.all_gather(jnp.concatenate([mine, cells], axis=0), 'sta')]
  transfers between devices with their start and end apart: 3 -> 0, of which waited for: 3 -> 0; matrix products, arithmetic and copies ran while one was open for 0% -> 0% of each run, Pallas kernels for 0% -> 0%
where the time goes in v2:
time: 72.6 us; the launch traced here: 71.6 us
  Pallas kernels  65.9 us (91%)
  local copies, waits for them, and re-layouts  4.34 us (6%)
    pallas_call x1, Pallas kernels, exchange_in(): pl.pallas_call(functools.partial(gather_kernel, owners, ranges, major), i...  29.4 us
    pallas_call x1, Pallas kernels, exchange_out(): pl.pallas_call(functools.partial(spread_kernel, ranges), in_specs=[pl.Blo...  15.9 us
    pallas_call x1, Pallas kernels, per_device(): pl.pallas_call(functools.partial(anomaly_kernel, ranges, cell_dev, cell_p...  7.84 us
    pallas_call x1, Pallas kernels, per_device(): pl.pallas_call(functools.partial(sums_kernel, ranges, packed), grid=(bloc...  7.33 us
    pallas_call x1, Pallas kernels, per_device(): pl.pallas_call(functools.partial(cells_kernel, ranges, packed, cell_dev,...  5.44 us
    unnamed x10, local copies, waits for them, and re-layouts  4.2 us

profile of v2, /device:TPU:0, one launch (start us, length us, event | category | flops | bytes accessed | tf_op | source)
XLA Modules:
  0.0 71.6 jit_solution(294146317801206318)
XLA Ops:
  0.6 0.7 fusion
  1.3 0.1 copy.7.own_ref
  1.5 0.0 copy-start
  1.5 1.9 %copy-done = f32[6144,128]{1,0:T(8,128)S(1)} copy-done((f32[6144,128]{1,0:T(8,128)S(1)}, f32[6144,128]{1,0:T(8,128)}, u32[]{:S(2)}) %copy-start) | copy-done | bytes 3145752
  3.4 0.0 copy-start.2
  3.4 0.9 %copy-done.2 = s32[4,6144]{1,0:T(4,128)S(1)} copy-done((s32[4,6144]{1,0:T(4,128)S(1)}, s32[4,6144]{1,0:T(4,128)}, u32[]{:S(2)}) %copy-start.2) | copy-done | bytes 98328
  4.3 0.0 copy-start.3
  4.3 0.7 %copy-done.3 = s32[6144]{0:T(1024)S(1)} copy-done((s32[6144]{0:T(1024)S(1)}, s32[6144]{0:T(1024)}, u32[]{:S(2)}) %copy-start.3) | copy-done | bytes 24600
  5.0 0.0 copy-start.4
  5.0 0.7 copy-done.4
  5.7 7.3 %shard_map.68.sums_ref = f32[4,256,128]{2,1,0:T(8,128)S(1)} custom-call(f32[6144,128]{1,0:T(8,128)S(1)} %copy-done, s32[4,6144]{1,0:T(4,128)S(1)} %copy-done.2, s32[1,6144]{1,0:T(1,128)S(1)} %bitcast.5, s32[1,256]{1,0:T(1,128)S(1)} %copy-done.4), custom_call_target="tpu_custom_call" | custom-call | tf_op jit(solution)/shard_map/pallas_call | solution.py:388
  13.0 29.4 %shard_map.69.got_ref = f32[8,264,128]{2,1,0:T(8,128)S(1)} custom-call(f32[4,256,128]{2,1,0:T(8,128)S(1)} %shard_map.68.sums_ref, f32[8,128]{1,0:T(8,128)S(1)} %pad.4.cells_ref), custom_call_target="tpu_custom_call" | custom-call | tf_op jit(solution)/shard_map/pallas_call | solution.py:293
  42.4 0.0 copy-start.1
  42.5 5.4 %shard_map.70.part_ref = f32[3,392,128]{2,1,0:T(8,128)S(1)} custom-call(f32[8,264,128]{2,1,0:T(8,128)S(1)} %shard_map.69.got_ref, s32[1,1]{1,0:T(1,128)} %bitcast.2.first_ref, f32[256,1]{1,0:T(8,128)S(1)} %copy.7.own_ref), custom_call_target="tpu_custom_call" | custom-call | tf_op jit(solution)/shard_map/pallas_call | solution.py:410
  47.9 15.9 %shard_map.71.clim_ref = f32[4,3,392,128]{3,2,1,0:T(8,128)S(1)} custom-call(f32[3,392,128]{2,1,0:T(8,128)S(1)} %shard_map.70.part_ref), custom_call_target="tpu_custom_call" | custom-call | tf_op jit(solution)/shard_map/pallas_call | solution.py:355
  63.8 0.0 copy-done.1
  63.8 7.8 %shard_map.72 = (f32[6144,128]{1,0:T(8,128)}, f32[1296,384]{1,0:T(8,128)}) custom-call(f32[6144,128]{1,0:T(8,128)S(1)} %copy-done.1, s32[4,6144]{1,0:T(4,128)S(1)} %copy-done.2, s32[1,6144]{1,0:T(1,128)S(1)} %bitcast.6, s32[1,256]{1,0:T(1,128)S(1)} %copy-done.4, f32[4,3,392,128]{3,2,1,0:T(8,128)S(1)} %shard_map.71.clim_ref), custom_call_target="tpu_custom_call" | custom-call | tf_op jit(solution)/shard_map/pallas_call | solution.py:425
  (1 shorter events, 0.0 us)
Async XLA Ops:
  1.5 1.9 %copy-start = (f32[6144,128]{1,0:T(8,128)S(1)}, f32[6144,128]{1,0:T(8,128)}, u32[]{:S(2)}) copy-start(f32[6144,128]{1,0:T(8,128)} %temps_ref.3) | copy-start | bytes 9437188
  3.4 0.9 %copy-start.2 = (s32[4,6144]{1,0:T(4,128)S(1)}, s32[4,6144]{1,0:T(4,128)}, u32[]{:S(2)}) copy-start(s32[4,6144]{1,0:T(4,128)} %bits_ref.3) | copy-start | bytes 294916
  4.3 0.7 %copy-start.3 = (s32[6144]{0:T(1024)S(1)}, s32[6144]{0:T(1024)}, u32[]{:S(2)}) copy-start(s32[6144]{0:T(1024)} %param.7) | copy-start | bytes 73732
  5.0 0.7 copy-start.4
  42.4 21.4 %copy-start.1 = (f32[6144,128]{1,0:T(8,128)S(1)}, f32[6144,128]{1,0:T(8,128)}, u32[]{:S(2)}) copy-start(f32[6144,128]{1,0:T(8,128)} %temps_ref.3) | copy-start | bytes 9437188

commit v3 on v2

--- a/solution.py
+++ b/solution.py
@@ -205,11 +205,17 @@
     )
 
 
-def greet(peers):
+def greet(peers, maybe=(), maybe_count=0):
     barrier = pltpu.get_barrier_semaphore()
     for where in peers:
         pl.semaphore_signal(barrier, inc=1, device_id=where, device_id_type=pl.DeviceIdType.MESH)
-    pl.semaphore_wait(barrier, len(peers))
+    for able, where in maybe:
+        @pl.when(able)
+        def _():
+            pl.semaphore_signal(
+                barrier, inc=1, device_id=where, device_id_type=pl.DeviceIdType.MESH
+            )
+    pl.semaphore_wait(barrier, len(peers) + maybe_count)
 
 
 def gather_kernel(
@@ -224,11 +230,40 @@
     partner = {"yr": chip * 2 + 1 - core}
     chip_at = [lax.rem(chip + k, chips) for k in range(chips)]
     chip_from = [lax.rem(chip + chips - k, chips) for k in range(chips)]
-    row_at = [lax.rem(row + k, major) for k in range(major)]
-    row_from = [lax.rem(row + major - k, major) for k in range(major)]
-    far = [{"sta": row_at[k] * minor + place} for k in range(1, major)]
-    near = [{"sta": row * minor + lax.rem(place + j, minor)} for j in range(1, minor)]
-    greet([partner] + [{"yr": c * 2 + core} for c in chip_at[1:]] + far + near)
+    near_peers = [{"sta": row * minor + lax.rem(place + j, minor)} for j in range(1, minor)]
+    can_up, can_down = row < major - 1, row > 0
+
+    def up(d):
+        block = out_ref.at[(row - (d - 1)) * minor + place]
+        return remote(
+            block, block, far_send.at[0, d - 1], far_recv.at[0, d - 1],
+            {"sta": (row + 1) * minor + place},
+        )
+
+    def down(d):
+        block = out_ref.at[(row + (d - 1)) * minor + place]
+        return remote(
+            block, block, far_send.at[1, d - 1], far_recv.at[1, d - 1],
+            {"sta": (row - 1) * minor + place},
+        )
+
+    def near(side, d):
+        block = out_ref.at[(row + (d if side else -d)) * minor + place]
+        return [
+            remote(
+                block, block, near_send.at[side, d, j], near_recv.at[side, d, j], near_peers[j]
+            )
+            for j in range(minor - 1)
+        ]
+
+    greet(
+        [partner] + [{"yr": c * 2 + core} for c in chip_at[1:]] + near_peers,
+        [
+            (can_up, {"sta": (row + 1) * minor + place}),
+            (can_down, {"sta": (row - 1) * minor + place}),
+        ],
+        (2 * (major - 1) - row) // major + (row + major - 1) // major,
+    )
 
     pairs = []
     for k in [*range(1, chips), 0]:
@@ -256,29 +291,41 @@
     out_ref[sta, :stations] = total
     out_ref[sta, stations:] = cells_ref[...]
 
-    sent = pairs + crossing
-    fars, nears = [], []
-    for k in range(1, major):
-        copy = remote(
-            out_ref.at[sta], out_ref.at[sta], far_send.at[k - 1], far_recv.at[k - 1], far[k - 1]
-        )
+    for able, copy_of in ((can_up, up), (can_down, down)):
+        @pl.when(able)
+        def _():
+            copy_of(1).start()
+    for copy in near(0, 0):
         copy.start()
-        fars.append(copy)
-    for k in range(major):
-        if k:
-            fars[k - 1].wait_recv()
-        block = row_from[k] * minor + place
-        for j in range(1, minor):
-            at = k * max(minor - 1, 1) + j - 1
-            copy = remote(
-                out_ref.at[block], out_ref.at[block], near_send.at[at], near_recv.at[at],
-                near[j - 1],
-            )
-            copy.start()
-            nears.append(copy)
-    for copy in nears:
-        copy.wait_recv()
-    for copy in sent + fars + nears:
+    for d in range(1, major):
+        for side, have, able, copy_of in (
+            (0, row >= d, can_up, up), (1, row + d < major, can_down, down)
+        ):
+            @pl.when(have)
+            def _():
+                copy_of(d).wait_recv()
+                if d + 1 < major:
+                    @pl.when(able)
+                    def _():
+                        copy_of(d + 1).start()
+                for copy in near(side, d):
+                    copy.start()
+    for copy in near(0, 0):
+        copy.wait()
+    for d in range(1, major):
+        for side, have, able, copy_of in (
+            (0, row >= d, can_up, up), (1, row + d < major, can_down, down)
+        ):
+            @pl.when(have)
+            def _():
+                for copy in near(side, d):
+                    copy.wait()
+            reach = (row >= d - 1) if side == 0 else (row + d - 1 < major)
+
+            @pl.when(reach & able)
+            def _():
+                copy_of(d).wait_send()
+    for copy in pairs + crossing:
         copy.wait_send()
 
 
@@ -288,7 +335,7 @@
     chips, minor = ranges // 2, owners // major
     block = stations + cells.shape[0]
     dma = pltpu.SemaphoreType.DMA
-    near_count = max(major * (minor - 1), 1)
+    hops, near_count = max(major - 1, 1), max(minor - 1, 1)
     crossings = max(chips - 1, 1)
     return pl.pallas_call(
         functools.partial(gather_kernel, owners, ranges, major),
@@ -300,7 +347,7 @@
             pltpu.VMEM((crossings, stations, LANES), F32),
             pltpu.VMEM((crossings, stations, LANES), F32),
             dma((chips,)), dma((chips,)), dma((crossings,)), dma((crossings,)),
-            dma((max(major - 1, 1),)), dma((max(major - 1, 1),)), dma((near_count,)), dma((near_count,)),
+            dma((2, hops)), dma((2, hops)), dma((2, major, near_count)), dma((2, major, near_count)),
         ],
         compiler_params=pltpu.CompilerParams(
             collective_id=0, has_side_effects=True, vmem_limit_bytes=48 * 1024 * 1024
@@ -385,6 +432,7 @@
     params = pltpu.CompilerParams(
         dimension_semantics=("arbitrary",), vmem_limit_bytes=48 * 1024 * 1024
     )
+    wide = pltpu.CompilerParams(dimension_semantics=("arbitrary",), vmem_limit_bytes=67043328)
     sums = pl.pallas_call(
         functools.partial(sums_kernel, ranges, packed),
         grid=(block_total // rows,),
@@ -395,7 +443,7 @@
             pltpu.VMEM((3 * stations, 3 * LANES), F32),
             pltpu.VMEM((2, stations, LANES), jnp.int32),
         ],
-        compiler_params=params,
+        compiler_params=wide,
     )(temps, day_bits, offsets, block_counts)
 
     cell_row_count = round_up(stations // LANES, 8)

time: 72.6 us -> 72.9 us (level)
  Pallas kernels: 65.9 us -> 67.2 us
    pallas_call x1, Pallas kernels: 7.33 us -> 9.25 us  [per_device(): pl.pallas_call(functools.partial(sums_kernel, ranges, packed), grid=(bloc...]
    unnamed x10 -> x14, local copies, waits for them, and re-layouts: 4.2 us -> 2.63 us
    pallas_call x1, Pallas kernels: 29.4 us -> 27.9 us  [exchange_in(): pl.pallas_call(functools.partial(gather_kernel, owners, ranges, major), i...]
    pallas_call x1, Pallas kernels: 15.9 us -> 16.8 us  [exchange_out(): pl.pallas_call(functools.partial(spread_kernel, ranges), in_specs=[pl.Blo...]
where the time goes in v3:
time: 72.9 us; the launch traced here: 72.6 us
  Pallas kernels  67.2 us (92%)
  local copies, waits for them, and re-layouts  4.02 us (6%)
    pallas_call x1, Pallas kernels, exchange_in(): pl.pallas_call(functools.partial(gather_kernel, owners, ranges, major), i...  27.9 us
    pallas_call x1, Pallas kernels, exchange_out(): pl.pallas_call(functools.partial(spread_kernel, ranges), in_specs=[pl.Blo...  16.8 us
    pallas_call x1, Pallas kernels, per_device(): pl.pallas_call(functools.partial(sums_kernel, ranges, packed), grid=(bloc...  9.25 us
    pallas_call x1, Pallas kernels, per_device(): pl.pallas_call(functools.partial(anomaly_kernel, ranges, cell_dev, cell_p...  7.84 us
    pallas_call x1, Pallas kernels, per_device(): pl.pallas_call(functools.partial(cells_kernel, ranges, packed, cell_dev,...  5.47 us
    unnamed x14, local copies, waits for them, and re-layouts  2.63 us

profile of v3, /device:TPU:0, one launch (start us, length us, event | category | flops | bytes accessed | tf_op | source)
XLA Modules:
  0.0 72.6 jit_solution(17326389220788164811)
XLA Ops:
  0.6 0.7 fusion
  1.3 0.6 pad.4.cells_ref
  1.9 0.8 %copy.7.own_ref = f32[256,1]{1,0:T(8,128)} copy(f32[256,1]{0,1:T(1,128)S(1)} %bitcast.7) | data formatting | bytes 2048 | tf_op jit(solution)/shard_map/reshape | solution.py:469
  2.7 9.3 %shard_map.68.sums_ref = f32[4,256,128]{2,1,0:T(8,128)} custom-call(f32[6144,128]{1,0:T(8,128)} %temps_ref.3, s32[4,6144]{1,0:T(4,128)} %bits_ref.3, s32[1,6144]{1,0:T(1,128)} %bitcast.5, s32[1,256]{1,0:T(1,128)} %counts_ref.3), custom_call_target="tpu_custom_call" | custom-call | tf_op jit(solution)/shard_map/pallas_call | solution.py:436
  12.0 0.0 copy-start.1
  12.0 1.0 %copy-done.1 = f32[4,256,128]{2,1,0:T(8,128)S(1)} copy-done((f32[4,256,128]{2,1,0:T(8,128)S(1)}, f32[4,256,128]{2,1,0:T(8,128)}, u32[]{:S(2)}) %copy-start.1) | copy-done | bytes 524312
  13.0 0.0 copy-start.5
  13.0 0.7 copy-done.5
  13.7 27.9 %shard_map.69.got_ref = f32[8,264,128]{2,1,0:T(8,128)S(1)} custom-call(f32[4,256,128]{2,1,0:T(8,128)S(1)} %copy-done.1, f32[8,128]{1,0:T(8,128)S(1)} %copy-done.5), custom_call_target="tpu_custom_call" | custom-call | tf_op jit(solution)/shard_map/pallas_call | solution.py:340
  41.6 0.0 copy-start.2
  41.6 0.9 %copy-done.2 = f32[256,1]{1,0:T(8,128)S(1)} copy-done((f32[256,1]{1,0:T(8,128)S(1)}, f32[256,1]{1,0:T(8,128)}, u32[]{:S(2)}) %copy-start.2) | copy-done | bytes 1048
  42.5 0.0 copy-start
  42.5 0.0 copy-start.3
  42.5 0.0 copy-start.4
  42.5 0.0 copy-start.6
  42.5 5.5 %shard_map.70.part_ref = f32[3,392,128]{2,1,0:T(8,128)S(1)} custom-call(f32[8,264,128]{2,1,0:T(8,128)S(1)} %shard_map.69.got_ref, s32[1,1]{1,0:T(1,128)} %bitcast.2.first_ref, f32[256,1]{1,0:T(8,128)S(1)} %copy-done.2), custom_call_target="tpu_custom_call" | custom-call | tf_op jit(solution)/shard_map/pallas_call | solution.py:458
  48.0 16.8 %shard_map.71.clim_ref = f32[4,3,392,128]{3,2,1,0:T(8,128)S(1)} custom-call(f32[3,392,128]{2,1,0:T(8,128)S(1)} %shard_map.70.part_ref), custom_call_target="tpu_custom_call" | custom-call | tf_op jit(solution)/shard_map/pallas_call | solution.py:402
  64.7 0.0 copy-done
  64.8 0.0 copy-done.3
  64.8 0.0 copy-done.4
  64.8 0.0 copy-done.6
  64.8 7.8 %shard_map.72 = (f32[6144,128]{1,0:T(8,128)}, f32[1296,384]{1,0:T(8,128)}) custom-call(f32[6144,128]{1,0:T(8,128)S(1)} %copy-done, s32[4,6144]{1,0:T(4,128)S(1)} %copy-done.3, s32[1,6144]{1,0:T(1,128)S(1)} %bitcast.6, s32[1,256]{1,0:T(1,128)S(1)} %copy-done.6, f32[4,3,392,128]{3,2,1,0:T(8,128)S(1)} %shard_map.71.clim_ref), custom_call_target="tpu_custom_call" | custom-call | tf_op jit(solution)/shard_map/pallas_call | solution.py:473
Async XLA Ops:
  12.0 1.0 %copy-start.1 = (f32[4,256,128]{2,1,0:T(8,128)S(1)}, f32[4,256,128]{2,1,0:T(8,128)}, u32[]{:S(2)}) copy-start(f32[4,256,128]{2,1,0:T(8,128)} %shard_map.68.sums_ref) | copy-start | bytes 1572868
  13.0 0.7 copy-start.5
  41.6 0.9 %copy-start.2 = (f32[256,1]{1,0:T(8,128)S(1)}, f32[256,1]{1,0:T(8,128)}, u32[]{:S(2)}) copy-start(f32[256,1]{1,0:T(8,128)} %copy.7.own_ref) | copy-start | bytes 3076
  42.5 22.3 %copy-start = (f32[6144,128]{1,0:T(8,128)S(1)}, f32[6144,128]{1,0:T(8,128)}, u32[]{:S(2)}) copy-start(f32[6144,128]{1,0:T(8,128)} %temps_ref.3) | copy-start | bytes 9437188
  42.5 22.3 %copy-start.3 = (s32[4,6144]{1,0:T(4,128)S(1)}, s32[4,6144]{1,0:T(4,128)}, u32[]{:S(2)}) copy-start(s32[4,6144]{1,0:T(4,128)} %bits_ref.3) | copy-start | bytes 294916
  42.5 22.3 %copy-start.4 = (s32[6144]{0:T(1024)S(1)}, s32[6144]{0:T(1024)}, u32[]{:S(2)}) copy-start(s32[6144]{0:T(1024)} %param.7) | copy-start | bytes 73732
  42.5 22.3 %copy-start.6 = (s32[1,256]{1,0:T(1,128)S(1)}, s32[1,256]{1,0:T(1,128)}, u32[]{:S(2)}) copy-start(s32[1,256]{1,0:T(1,128)} %counts_ref.3) | copy-start | bytes 3076

commit v4 on v3

--- a/solution.py
+++ b/solution.py
@@ -93,12 +93,27 @@
             out_ref[r] = gather_lanes(groups, [width * (k - r) for k in range(len(groups))], width)
 
 
-def cells_kernel(ranges, packed, cell_dev, cell_pad, got_ref, first_ref, own_ref, out_ref, acc):
+def cell_chunks(ranges, cell_pad, stations):
+    cell_rows, station_rows = cell_pad // ranges, stations // ranges
+    step = round_up((cell_rows + 2) // 3, 8)
+    edges = [*range(0, cell_rows, step), cell_rows]
+    return [(cell_rows, cell_rows + station_rows)] + list(zip(edges[:-1], edges[1:]))
+
+
+def cells_kernel(
+    ranges, packed, cell_dev, cell_pad, got_ref, own_ref, out_ref, values, acc,
+    far_send, far_recv, near_send, near_recv,
+):
     shards, _, _ = got_ref.shape
     stations = own_ref.shape[0]
     width = LANES // ranges
-    ids = lax.broadcasted_iota(jnp.int32, (cell_pad, 1), 0).astype(F32) + first_ref[0, 0].astype(F32)
-    acc[...] = jnp.zeros_like(acc)
+    chips = ranges // 2
+    yr = lax.axis_index("yr")
+    chip, core = yr // 2, lax.rem(yr, 2)
+    partner = {"yr": chip * 2 + 1 - core}
+    others = [lax.rem(chip + k, chips) * 2 + core for k in range(1, chips)]
+    origins = [lax.rem(chip + chips - k, chips) * 2 + core for k in range(1, chips)]
+    greet([partner] + [{"yr": other} for other in others])
     group = lane_group(stations, width)
     for s in range(shards):
         both = got_ref[s, :stations, :]
@@ -114,32 +129,68 @@
                     (pltpu.roll(tally, LANES - width, 1) >> 16) & 255,
                 ),
             ).astype(F32)
-            values = [high, low, tally.astype(BF16)]
+            columns = [high, low, tally.astype(BF16)]
         else:
             tally = pltpu.roll(both, LANES - 3 * width, 1)
-            values = [high, low, *split_two(tally)]
-        values = jnp.concatenate(values, axis=1)
-        for q in range(stations // LANES):
-            cells = got_ref[s, stations + q : stations + q + 1, :]
-            part = values[q * LANES : (q + 1) * LANES]
-            hot = jnp.where(ids == cells, 1.0, 0.0).astype(BF16)
-            acc[:cell_pad] += jnp.dot(hot, part, preferred_element_type=F32)
-            hot = jnp.where(own_ref[...] == cells, 1.0, 0.0).astype(BF16)
-            acc[cell_pad:] += jnp.dot(hot, part, preferred_element_type=F32)
-    tallies = acc[:, 2 * LANES : 3 * LANES]
-    if not packed:
-        tallies = tallies + acc[:, 3 * LANES :]
-    acc[:, :LANES] = (acc[:, :LANES] + acc[:, LANES : 2 * LANES]) / jnp.maximum(tallies, 1.0)
-    cell_rows, station_rows = cell_pad // ranges, stations // ranges
-    for k in range(3):
-        shifts = [width * (j - k) for j in range(ranges)]
-        out_ref[k, :cell_rows] = gather_lanes(
-            [acc[j * cell_rows : (j + 1) * cell_rows, :LANES] for j in range(ranges)], shifts, width
-        )
-        first = [cell_pad + j * station_rows for j in range(ranges)]
-        out_ref[k, cell_rows:] = gather_lanes(
-            [acc[f : f + station_rows, :LANES] for f in first], shifts, width
-        )
+            columns = [high, low, *split_two(tally)]
+        values[s * stations : (s + 1) * stations] = jnp.concatenate(columns, axis=1)
+    first = lax.axis_index("sta") * cell_dev
+    cell_rows = cell_pad // ranges
+    fars, nears = [], []
+    for c, (low_row, high_row) in enumerate(cell_chunks(ranges, cell_pad, stations)):
+        count = high_row - low_row
+        if low_row == cell_rows:
+            ids = own_ref[...]
+        else:
+            ids = jnp.concatenate(
+                [
+                    lax.broadcasted_iota(jnp.int32, (count, 1), 0) + (first + j * cell_rows + low_row)
+                    for j in range(ranges)
+                ],
+                axis=0,
+            ).astype(F32)
+        total = ranges * count
+        acc[:total] = jnp.zeros((total, acc.shape[1]), F32)
+        for s in range(shards):
+            hot = jnp.concatenate(
+                [
+                    jnp.where(ids == got_ref[s, q : q + 1, :], 1.0, 0.0).astype(BF16)
+                    for q in range(stations, stations + stations // LANES)
+                ],
+                axis=1,
+            )
+            acc[:total] += jnp.dot(
+                hot, values[s * stations : (s + 1) * stations], preferred_element_type=F32
+            )
+        tallies = acc[:total, 2 * LANES : 3 * LANES]
+        if not packed:
+            tallies = tallies + acc[:total, 3 * LANES :]
+        clim = (acc[:total, :LANES] + acc[:total, LANES : 2 * LANES]) / jnp.maximum(tallies, 1.0)
+        for k in range(3):
+            out_ref[yr, k, low_row:high_row] = gather_lanes(
+                [clim[j * count : (j + 1) * count] for j in range(ranges)],
+                [width * (j - k) for j in range(ranges)],
+                width,
+            )
+        block = out_ref.at[yr, :, low_row:high_row, :]
+        for k, other in enumerate(others):
+            copy = remote(block, block, far_send.at[c, k], far_recv.at[c, k], {"yr": other})
+            copy.start()
+            fars.append(copy)
+        copy = remote(block, block, near_send.at[c, chips - 1], near_recv.at[c, chips - 1], partner)
+        copy.start()
+        nears.append(copy)
+    for c, (low_row, high_row) in enumerate(cell_chunks(ranges, cell_pad, stations)):
+        for k, origin in enumerate(origins):
+            fars[c * len(origins) + k].wait_recv()
+            block = out_ref.at[origin, :, low_row:high_row, :]
+            copy = remote(block, block, near_send.at[c, k], near_recv.at[c, k], partner)
+            copy.start()
+            nears.append(copy)
+    for copy in nears:
+        copy.wait_recv()
+    for copy in fars + nears:
+        copy.wait_send()
 
 
 def unpack(clim_ref, k, j, first, count, ranges, width):
@@ -355,65 +406,6 @@
     )(sums, cells)
 
 
-def spread_kernel(ranges, part_ref, out_ref, far_send, far_recv, near_send, near_recv):
-    chips = ranges // 2
-    chunks = part_ref.shape[0]
-    yr = lax.axis_index("yr")
-    chip, core = yr // 2, lax.rem(yr, 2)
-    partner = {"yr": chip * 2 + 1 - core}
-    others = [lax.rem(chip + k, chips) * 2 + core for k in range(1, chips)]
-    origins = [lax.rem(chip + chips - k, chips) * 2 + core for k in range(1, chips)]
-    greet([partner] + [{"yr": other} for other in others])
-    fars, nears = [], []
-    for t in range(chunks):
-        for k, other in enumerate(others):
-            at = t * len(others) + k
-            copy = remote(
-                part_ref.at[t], out_ref.at[yr, t], far_send.at[at], far_recv.at[at], {"yr": other}
-            )
-            copy.start()
-            fars.append(copy)
-    for t in range(chunks):
-        copy = remote(part_ref.at[t], out_ref.at[yr, t], near_send.at[t], near_recv.at[t], partner)
-        copy.start()
-        nears.append(copy)
-    out_ref[yr] = part_ref[...]
-    for t in range(chunks):
-        for k, origin in enumerate(origins):
-            at = t * len(others) + k
-            fars[at].wait_recv()
-            at = chunks + at
-            copy = remote(
-                out_ref.at[origin, t], out_ref.at[origin, t], near_send.at[at], near_recv.at[at],
-                partner,
-            )
-            copy.start()
-            nears.append(copy)
-    for copy in nears:
-        copy.wait_recv()
-    for copy in fars + nears:
-        copy.wait_send()
-
-
-def exchange_out(part, ranges):
-    chunks = part.shape[0]
-    crossings = chunks * (ranges // 2 - 1)
-    dma = pltpu.SemaphoreType.DMA
-    return pl.pallas_call(
-        functools.partial(spread_kernel, ranges),
-        in_specs=[pl.BlockSpec(memory_space=pltpu.VMEM)],
-        out_specs=pl.BlockSpec(memory_space=pltpu.VMEM),
-        out_shape=jax.ShapeDtypeStruct((ranges, *part.shape), F32),
-        scratch_shapes=[
-            dma((max(crossings, 1),)), dma((max(crossings, 1),)),
-            dma((chunks + crossings,)), dma((chunks + crossings,)),
-        ],
-        compiler_params=pltpu.CompilerParams(
-            collective_id=1, has_side_effects=True, vmem_limit_bytes=48 * 1024 * 1024
-        ),
-    )(part)
-
-
 def per_device(temps, day_bits, block_offset, block_counts, station_cell):
     owners, ranges = lax.axis_size("sta"), lax.axis_size("yr")
     stations = station_cell.shape[0]
@@ -432,7 +424,6 @@
     params = pltpu.CompilerParams(
         dimension_semantics=("arbitrary",), vmem_limit_bytes=48 * 1024 * 1024
     )
-    wide = pltpu.CompilerParams(dimension_semantics=("arbitrary",), vmem_limit_bytes=67043328)
     sums = pl.pallas_call(
         functools.partial(sums_kernel, ranges, packed),
         grid=(block_total // rows,),
@@ -443,7 +434,7 @@
             pltpu.VMEM((3 * stations, 3 * LANES), F32),
             pltpu.VMEM((2, stations, LANES), jnp.int32),
         ],
-        compiler_params=wide,
+        compiler_params=params,
     )(temps, day_bits, offsets, block_counts)
 
     cell_row_count = round_up(stations // LANES, 8)
@@ -453,22 +444,27 @@
     )
     got = exchange_in(sums, cell_rows, owners, ranges)
 
-    first = (lax.axis_index("sta") * cell_dev).astype(jnp.int32).reshape(1, 1)
     part_rows = (cell_pad + stations) // ranges
-    part = pl.pallas_call(
+    chunks = cell_chunks(ranges, cell_pad, stations)
+    most = max(high - low for low, high in chunks)
+    columns = (3 if packed else 4) * LANES
+    dma = pltpu.SemaphoreType.DMA
+    hops = (len(chunks), max(ranges // 2 - 1, 1))
+    steps = (len(chunks), ranges // 2)
+    parts = pl.pallas_call(
         functools.partial(cells_kernel, ranges, packed, cell_dev, cell_pad),
-        in_specs=[
-            pl.BlockSpec(memory_space=pltpu.VMEM),
-            pl.BlockSpec(memory_space=pltpu.SMEM),
-            pl.BlockSpec(memory_space=pltpu.VMEM),
-        ],
+        in_specs=[pl.BlockSpec(memory_space=pltpu.VMEM)] * 2,
         out_specs=pl.BlockSpec(memory_space=pltpu.VMEM),
-        out_shape=jax.ShapeDtypeStruct((3, part_rows, LANES), F32),
-        scratch_shapes=[pltpu.VMEM((cell_pad + stations, (3 if packed else 4) * LANES), F32)],
-        compiler_params=pltpu.CompilerParams(vmem_limit_bytes=48 * 1024 * 1024),
-    )(got, first, station_cell.astype(F32).reshape(stations, 1))
-
-    parts = exchange_out(part, ranges)
+        out_shape=jax.ShapeDtypeStruct((ranges, 3, part_rows, LANES), F32),
+        scratch_shapes=[
+            pltpu.VMEM((owners * stations, columns), BF16),
+            pltpu.VMEM((ranges * most, columns), F32),
+            dma(hops), dma(hops), dma(steps), dma(steps),
+        ],
+        compiler_params=pltpu.CompilerParams(
+            collective_id=1, has_side_effects=True, vmem_limit_bytes=48 * 1024 * 1024
+        ),
+    )(got, station_cell.astype(F32).reshape(stations, 1))
 
     return pl.pallas_call(
         functools.partial(anomaly_kernel, ranges, cell_dev, cell_pad),

time: 72.9 us -> 67.3 us (0.923)
  Pallas kernels: 67.2 us -> 61.3 us
    pallas_call x1 -> x0, Pallas kernels: 16.8 us -> none  [exchange_out(): pl.pallas_call(functools.partial(spread_kernel, ranges), in_specs=[pl.Blo...]
    pallas_call x1, Pallas kernels: 5.47 us -> 18.2 us  [per_device(): pl.pallas_call(functools.partial(cells_kernel, ranges, packed, cell_dev,...]
    pallas_call x1, Pallas kernels: 9.25 us -> 7.31 us  [per_device(): pl.pallas_call(functools.partial(sums_kernel, ranges, packed), grid=(bloc...]
    unnamed x14 -> x10, local copies, waits for them, and re-layouts: 2.63 us -> 4.2 us
where the time goes in v4:
time: 67.3 us; the launch traced here: 67 us
  Pallas kernels  61.3 us (91%)
  local copies, waits for them, and re-layouts  4.34 us (6%)
  between operations  0.69 us (1%)
  other arithmetic  0.68 us (1%)
    pallas_call x1, Pallas kernels, exchange_in(): pl.pallas_call(functools.partial(gather_kernel, owners, ranges, major), i...  27.9 us
    pallas_call x1, Pallas kernels, per_device(): pl.pallas_call(functools.partial(cells_kernel, ranges, packed, cell_dev,...  18.2 us
    pallas_call x1, Pallas kernels, per_device(): pl.pallas_call(functools.partial(anomaly_kernel, ranges, cell_dev, cell_p...  7.84 us
    pallas_call x1, Pallas kernels, per_device(): pl.pallas_call(functools.partial(sums_kernel, ranges, packed), grid=(bloc...  7.31 us
    unnamed x10, local copies, waits for them, and re-layouts  4.2 us

profile of v4, /device:TPU:0, one launch (start us, length us, event | category | flops | bytes accessed | tf_op | source)
XLA Modules:
  0.0 67.0 jit_solution(12944532487153054005)
XLA Ops:
  0.6 0.7 %fusion = (f32[256]{0:T(256)S(1)}, f32[2,128]{1,0:T(2,128)S(1)}) fusion(s32[256]{0:T(256)} %param.9), kind=kLoop, calls=%fused_computation.1 | loop fusion | flops 256 | bytes 3072 | tf_op jit(solution)/shard_map/convert_element_type | solution.py:442
  1.3 0.1 copy.7.own_ref
  1.5 0.0 copy-start
  1.5 1.9 %copy-done = f32[6144,128]{1,0:T(8,128)S(1)} copy-done((f32[6144,128]{1,0:T(8,128)S(1)}, f32[6144,128]{1,0:T(8,128)}, u32[]{:S(2)}) %copy-start) | copy-done | bytes 3145752
  3.4 0.0 copy-start.2
  3.4 0.9 %copy-done.2 = s32[4,6144]{1,0:T(4,128)S(1)} copy-done((s32[4,6144]{1,0:T(4,128)S(1)}, s32[4,6144]{1,0:T(4,128)}, u32[]{:S(2)}) %copy-start.2) | copy-done | bytes 98328
  4.2 0.0 copy-start.3
  4.3 0.7 %copy-done.3 = s32[6144]{0:T(1024)S(1)} copy-done((s32[6144]{0:T(1024)S(1)}, s32[6144]{0:T(1024)}, u32[]{:S(2)}) %copy-start.3) | copy-done | bytes 24600
  5.0 0.0 copy-start.4
  5.0 0.7 %copy-done.4 = s32[1,256]{1,0:T(1,128)S(1)} copy-done((s32[1,256]{1,0:T(1,128)S(1)}, s32[1,256]{1,0:T(1,128)}, u32[]{:S(2)}) %copy-start.4) | copy-done | bytes 1048
  5.7 7.3 %shard_map.68.sums_ref = f32[4,256,128]{2,1,0:T(8,128)S(1)} custom-call(f32[6144,128]{1,0:T(8,128)S(1)} %copy-done, s32[4,6144]{1,0:T(4,128)S(1)} %copy-done.2, s32[1,6144]{1,0:T(1,128)S(1)} %bitcast.4, s32[1,256]{1,0:T(1,128)S(1)} %copy-done.4), custom_call_target="tpu_custom_call" | custom-call | tf_op jit(solution)/shard_map/pallas_call | solution.py:427
  13.0 0.0 copy-start.1
  13.0 27.9 %shard_map.69.got_ref = f32[8,264,128]{2,1,0:T(8,128)S(1)} custom-call(f32[4,256,128]{2,1,0:T(8,128)S(1)} %shard_map.68.sums_ref, f32[8,128]{1,0:T(8,128)S(1)} %pad.4.cells_ref), custom_call_target="tpu_custom_call" | custom-call | tf_op jit(solution)/shard_map/pallas_call | solution.py:391
  40.9 18.2 %shard_map.70.clim_ref = f32[4,3,392,128]{3,2,1,0:T(8,128)S(1)} custom-call(f32[8,264,128]{2,1,0:T(8,128)S(1)} %shard_map.69.got_ref, f32[256,1]{1,0:T(8,128)S(1)} %copy.7.own_ref), custom_call_target="tpu_custom_call" | custom-call | tf_op jit(solution)/shard_map/pallas_call | solution.py:454
  59.1 0.0 copy-done.1
  59.2 7.8 %shard_map.71 = (f32[6144,128]{1,0:T(8,128)}, f32[1296,384]{1,0:T(8,128)}) custom-call(f32[6144,128]{1,0:T(8,128)S(1)} %copy-done.1, s32[4,6144]{1,0:T(4,128)S(1)} %copy-done.2, s32[1,6144]{1,0:T(1,128)S(1)} %bitcast.5, s32[1,256]{1,0:T(1,128)S(1)} %copy-done.4, f32[4,3,392,128]{3,2,1,0:T(8,128)S(1)} %shard_map.70.clim_ref), custom_call_target="tpu_custom_call" | custom-call | tf_op jit(solution)/shard_map/pallas_call | solution.py:469
  (1 shorter events, 0.0 us)
Async XLA Ops:
  1.5 1.9 %copy-start = (f32[6144,128]{1,0:T(8,128)S(1)}, f32[6144,128]{1,0:T(8,128)}, u32[]{:S(2)}) copy-start(f32[6144,128]{1,0:T(8,128)} %temps_ref.3) | copy-start | bytes 9437188
  3.4 0.9 %copy-start.2 = (s32[4,6144]{1,0:T(4,128)S(1)}, s32[4,6144]{1,0:T(4,128)}, u32[]{:S(2)}) copy-start(s32[4,6144]{1,0:T(4,128)} %bits_ref.3) | copy-start | bytes 294916
  4.2 0.7 %copy-start.3 = (s32[6144]{0:T(1024)S(1)}, s32[6144]{0:T(1024)}, u32[]{:S(2)}) copy-start(s32[6144]{0:T(1024)} %param.7) | copy-start | bytes 73732
  5.0 0.7 %copy-start.4 = (s32[1,256]{1,0:T(1,128)S(1)}, s32[1,256]{1,0:T(1,128)}, u32[]{:S(2)}) copy-start(s32[1,256]{1,0:T(1,128)} %counts_ref.3) | copy-start | bytes 3076
  13.0 46.2 %copy-start.1 = (f32[6144,128]{1,0:T(8,128)S(1)}, f32[6144,128]{1,0:T(8,128)}, u32[]{:S(2)}) copy-start(f32[6144,128]{1,0:T(8,128)} %temps_ref.3) | copy-start | bytes 9437188
